TPU v7x, 64 devices: a 2x2x8 block of a 4x4x8 slice. The times are simulated.
64 devices in a mesh: rep: 4 (over x, y), data: 16 (over z, core).
Axes of the slice: x: 2, y: 2, z: 8, core: 2. Of those that a mesh axis runs over, the one named last changes fastest.
The devices are a block of a 4x4x8 slice.
Arguments:
- hidden: bfloat16 [8192, 1536], P(('rep', 'data')), parts along dimension 0
- adapter_id: int32 [8192], P(('rep', 'data')), parts along dimension 0
- w_gate: bfloat16 [1536, 8960], replicated
- w_up: bfloat16 [1536, 8960], replicated
- w_down: bfloat16 [8960, 1536], replicated
- a_gate: bfloat16 [128, 1536, 16], replicated
- b_gate: bfloat16 [128, 16, 8960], P('data')
- a_up: bfloat16 [128, 1536, 16], replicated
- b_up: bfloat16 [128, 16, 8960], P('data')
- a_down: bfloat16 [128, 8960, 16], replicated
- b_down: bfloat16 [128, 16, 1536], P('data')
Outputs:
- output: bfloat16 [8192, 1536], P(('rep', 'data')), parts along dimension 0
There are 4 independent parts. A program takes and returns all parts, laid end to end along the dimension named above; an argument that names none is the same for every part.
All inputs are finite; a program needn't handle non-finite values.
Results may differ from a plain program's by a relative error of at most 0.00623724.
Values are sent between devices in bfloat16 or wider.
A program may use at most 768 MiB of HBM per device.

v0:
```python
import jax
import jax.numpy as jnp
from jax import lax
from jax.sharding import PartitionSpec as P

value_a10 = 2.0


def pick_low(act_rows, a_all, adapter_hot):
    all_low = jnp.einsum('tk,akr->tar', act_rows, a_all, preferred_element_type=jnp.float32)
    return jnp.sum(all_low * adapter_hot[:, :, None], axis=1).astype(jnp.bfloat16)


def value_a7(low_rows, local_hot, b_local):
    spread = local_hot[:, :, None] * low_rows[:, None, :]
    delta_out = jnp.einsum('mar,arf->mf', spread, b_local, preferred_element_type=jnp.float32)
    return (value_a10 * delta_out).astype(jnp.bfloat16)


def solution(mesh):
    groups = mesh.shape['data']
    row_spec = P(('rep', 'data'), None)
    tok_spec = P(('rep', 'data'))
    full_two = P(None, None)
    full_three = P(None, None, None)
    owned = P('data', None, None)

    def device_fn(hidden, adapter_id, w_gate, w_up, w_down, a_gate, b_gate, a_up, b_up, a_down, b_down):
        tok_local = hidden.shape[0]
        adapters = a_gate.shape[0]
        per_owner = b_gate.shape[0]
        value_a9 = a_gate.shape[2]
        capacity = min(4 * tok_local // groups, tok_local // 2)
        owner_ids = adapter_id // per_owner
        owner_hot = (owner_ids[:, None] == jnp.arange(groups)[None, :]).astype(jnp.int32)
        slot_rank = jnp.sum(jnp.cumsum(owner_hot, axis=0) * owner_hot, axis=1) - 1
        flat_slot = owner_ids * capacity + slot_rank
        adapter_hot = (adapter_id[:, None] == jnp.arange(adapters)[None, :]).astype(jnp.float32)

        send_ids = jnp.full((groups * capacity,), -1, jnp.int32).at[flat_slot].set(adapter_id % per_owner)
        recv_ids = lax.all_to_all(send_ids, 'data', 0, 0, tiled=True)
        local_hot = (recv_ids[:, None] == jnp.arange(per_owner)[None, :]).astype(jnp.bfloat16)

        low_both = jnp.concatenate([pick_low(hidden, a_gate, adapter_hot), pick_low(hidden, a_up, adapter_hot)], axis=1)
        send_low = jnp.zeros((groups * capacity, 2 * value_a9), jnp.bfloat16).at[flat_slot].set(low_both)
        recv_low = lax.all_to_all(send_low, 'data', 0, 0, tiled=True)
        delta_gate = value_a7(recv_low[:, :value_a9], local_hot, b_gate)
        delta_up = value_a7(recv_low[:, value_a9:], local_hot, b_up)
        back_gate = lax.all_to_all(delta_gate, 'data', 0, 0, tiled=True)
        back_up = lax.all_to_all(delta_up, 'data', 0, 0, tiled=True)

        gate_act = jnp.dot(hidden, w_gate, preferred_element_type=jnp.float32) + jnp.take(back_gate, flat_slot, axis=0).astype(jnp.float32)
        up_act = jnp.dot(hidden, w_up, preferred_element_type=jnp.float32) + jnp.take(back_up, flat_slot, axis=0).astype(jnp.float32)
        hid_act = (jax.nn.silu(gate_act) * up_act).astype(jnp.bfloat16)

        send_down = jnp.zeros((groups * capacity, value_a9), jnp.bfloat16).at[flat_slot].set(pick_low(hid_act, a_down, adapter_hot))
        recv_down = lax.all_to_all(send_down, 'data', 0, 0, tiled=True)
        back_down = lax.all_to_all(value_a7(recv_down, local_hot, b_down), 'data', 0, 0, tiled=True)
        down_act = jnp.dot(hid_act, w_down, preferred_element_type=jnp.float32) + jnp.take(back_down, flat_slot, axis=0).astype(jnp.float32)
        return (hidden.astype(jnp.float32) + down_act).astype(jnp.bfloat16)

    return jax.shard_map(device_fn, mesh=mesh, in_specs=(row_spec, tok_spec, full_two, full_two, full_two, full_three, owned, full_three, owned, full_three, owned), out_specs=row_spec, check_vma=False)
```

profile of v0, /device:TPU:21, one launch (start us, length us, event | category | flops | bytes accessed | tf_op | source)
XLA Modules:
  0.0 629.0 jit_solution(12302783830436175597)
XLA Ops:
  0.0 0.0 copy-start
  0.0 0.8 and_select_fusion
  0.8 0.1 fusion.52
  0.9 0.2 reduce_window_sum.11
  1.1 0.2 select_reduce_fusion
  1.3 1.0 scatter_custom_fusion
  2.3 0.7 all_to_all.44
  2.9 10.7 %all-to-all-start = ((s32[16,32,1]{1,2,0:T(1,128)}), s32[16,32,1]{1,2,0:T(1,128)S(1)}, u32[]{:S(2)}, u32[]{:S(2)}) async-start(s32[16,32,1]{1,2,0:T(1,128)} %bitcast), calls=%async_computation | async-start | bytes 16384 | tf_op jit(solution)/shard_map/all_to_all | solution.py:41
  13.7 0.7 fusion.53
  14.3 0.0 copy-start.4
  14.3 0.0 copy-start.5
  14.3 10.0 %fusion.31 = bf16[128,16]{0,1:T(8,128)(2,1)S(1)} fusion(bf16[128,1536,16]{1,2,0:T(8,128)(2,1)} %param.20, f32[128,128]{0,1:T(8,128)S(1)} %fusion.53, bf16[128,1536]{1,0:T(8,128)(2,1)} %param.13), kind=kOutput, calls=%fused_computation.31 | convolution fusion | flops 805828608 | bytes 6754304 | tf_op jit(solution)/shard_map/tk,akr->tar/dot_general | solution.py:10
  24.3 0.0 copy-done.4
  24.3 0.0 copy-done.5
  24.4 7.6 %fusion.34 = bf16[128,16]{0,1:T(8,128)(2,1)S(1)} fusion(bf16[128,1536,16]{1,2,0:T(8,128)(2,1)S(1)} %copy-done.5, f32[128,128]{0,1:T(8,128)S(1)} %fusion.53, bf16[128,1536]{1,0:T(8,128)(2,1)S(1)} %copy-done.4), kind=kOutput, calls=%fused_computation.32 | convolution fusion | flops 805828608 | bytes 6754304 | tf_op jit(solution)/shard_map/tk,akr->tar/dot_general | solution.py:10
  31.9 0.1 copy.33
  32.0 0.9 scatter_custom_fusion.1
  33.0 0.8 reshape.153
  33.7 0.0 all-to-all-done
  33.8 7.2 %all-to-all-start.1 = ((bf16[16,2,512]{2,1,0:T(2,128)(2,1)}), bf16[16,2,512]{2,1,0:T(2,128)(2,1)S(1)}, u32[]{:S(2)}, u32[]{:S(2)}) async-start(bf16[16,2,512]{2,1,0:T(2,128)(2,1)} %reshape.153), calls=%async_computation.1 | async-start | bytes 65536 | tf_op jit(solution)/shard_map/all_to_all | solution.py:46
  41.0 0.6 broadcast.97
  41.6 0.7 reduce.3
  42.3 0.1 eq.54
  42.4 5.7 all-to-all-done.1
  48.1 0.1 reshape.154
  48.3 0.1 fusion.57
  48.4 0.1 copy.40
  48.5 0.0 copy-done
  48.5 6.1 fusion.3
  54.6 0.0 copy-start.6
  54.6 5.0 all-to-all-start.2
  59.7 0.1 copy.41
  59.7 0.0 copy-done.6
  59.7 6.2 fusion.2
  65.9 200.9 %all-to-all-done.2 = bf16[16,32,8960]{2,1,0:T(8,128)(2,1)} async-done(((bf16[16,32,8960]{2,1,0:T(8,128)(2,1)}), bf16[16,32,8960]{2,1,0:T(8,128)(2,1)}, u32[]{:S(2)}, u32[]{:S(2)}) %all-to-all-start.2) | async-done | bytes 9175072 | tf_op jit(solution)/shard_map/all_to_all | solution.py:49
  266.8 8.3 %all-to-all-start.3 = ((bf16[16,32,8960]{2,1,0:T(8,128)(2,1)}), bf16[16,32,8960]{2,1,0:T(8,128)(2,1)}, u32[]{:S(2)}, u32[]{:S(2)}) async-start(bf16[16,32,8960]{2,1,0:T(8,128)(2,1)} %bitcast.54), calls=%async_computation.3 | async-start | bytes 18350080 | tf_op jit(solution)/shard_map/all_to_all | solution.py:50
  275.1 8.8 %gather_fusion.1 = bf16[128,8960]{1,0:T(8,128)(2,1)S(1)} fusion(bf16[512,8960]{1,0:T(8,128)(2,1)} %bitcast.6, s32[1024]{0:T(1024)S(1)} %pad_clamp_fusion), kind=kCustom, calls=%fused_computation.clone | custom fusion | bytes 4588032 | tf_op jit(solution)/shard_map/jit(_take)/gather | solution.py:52
  284.0 197.5 %all-to-all-done.3 = bf16[16,32,8960]{2,1,0:T(8,128)(2,1)} async-done(((bf16[16,32,8960]{2,1,0:T(8,128)(2,1)}), bf16[16,32,8960]{2,1,0:T(8,128)(2,1)}, u32[]{:S(2)}, u32[]{:S(2)}) %all-to-all-start.3) | async-done | bytes 9175072 | tf_op jit(solution)/shard_map/all_to_all | solution.py:50
  481.5 10.2 %gather_fusion.2 = bf16[128,8960]{1,0:T(8,128)(2,1)} fusion(bf16[512,8960]{1,0:T(8,128)(2,1)} %bitcast.9, s32[1024]{0:T(1024)S(1)} %pad_clamp_fusion), kind=kCustom, calls=%fused_computation.1.clone | custom fusion | bytes 4588032 | tf_op jit(solution)/shard_map/jit(_take)/gather | solution.py:53
  491.8 0.0 copy-start.3
  491.8 11.1 %convolution_add_fusion.1 = f32[128,8960]{1,0:T(8,128)S(1)} fusion(bf16[128,1536]{1,0:T(8,128)(2,1)S(1)} %copy-done.4, bf16[1536,8960]{1,0:T(8,128)(2,1)} %param.15, bf16[128,8960]{1,0:T(8,128)(2,1)S(1)} %gather_fusion.1, pred[128]{0:T(512)(128)(4,1)S(1)} %get-tuple-element.6), kind=kOutput, calls=%fused_computation.14 | convolution fusion | flops 3526656000 | bytes 34799744 | tf_op jit(solution)/shard_map/dot_general | solution.py:52
  502.8 0.0 copy-done.3
  502.8 11.7 %fusion.5 = bf16[128,8960]{1,0:T(8,128)(2,1)S(1)} fusion(bf16[128,1536]{1,0:T(8,128)(2,1)S(1)} %copy-done.4, bf16[1536,8960]{1,0:T(8,128)(2,1)} %param.16, f32[128,8960]{1,0:T(8,128)S(1)} %convolution_add_fusion.1, bf16[128,8960]{1,0:T(8,128)(2,1)S(1)} %copy-done.3, pred[128]{0:T(512)(128)(4,1)S(1)} %get-tuple-element.6), kind=kOutput, calls=%fused_computation.15 | convolution fusion | flops 3533537280 | bytes 37093504 | tf_op jit(solution)/shard_map/dot_general | solution.py:53
  514.5 0.0 copy-start.2
  514.5 38.6 %fusion.26 = bf16[128,16]{0,1:T(8,128)(2,1)S(1)} fusion(bf16[128,8960,16]{1,2,0:T(8,128)(2,1)} %param.22, bf16[128,8960]{1,0:T(8,128)(2,1)S(1)} %fusion.5, f32[128,128]{0,1:T(8,128)S(1)} %fusion.53), kind=kOutput, calls=%fused_computation.30 | convolution fusion | flops 4698142720 | bytes 39063552 | tf_op jit(solution)/shard_map/tk,akr->tar/dot_general | solution.py:10
  553.2 0.0 copy-done.2
  553.2 0.1 copy.37
  553.3 0.9 scatter_custom_fusion.2
  554.3 0.1 copy.38
  554.4 0.1 reshape.155
  554.5 15.0 %all_to_all.66 = bf16[16,2,256]{2,1,0:T(2,128)(2,1)S(1)} all-to-all(bf16[16,2,256]{2,1,0:T(2,128)(2,1)S(1)} %reshape.155), channel_id=1, replica_groups=mesh['rep'=4,'data'=16] {'data'}, dimensions={0} | all-to-all | bytes 32768 | tf_op jit(solution)/shard_map/all_to_all | solution.py:57
  569.4 0.1 reshape.156
  569.6 0.1 mul.101
  569.7 1.6 fusion.11
  571.3 42.2 %all_to_all.67 = bf16[16,32,1536]{2,1,0:T(8,128)(2,1)S(1)} all-to-all(bf16[16,32,1536]{2,1,0:T(8,128)(2,1)S(1)} %bitcast.56), channel_id=1, replica_groups=mesh['rep'=4,'data'=16] {'data'}, dimensions={0} | all-to-all | bytes 3145728 | tf_op jit(solution)/shard_map/all_to_all | solution.py:58
  613.5 0.9 gather_fusion
  614.4 0.0 copy-start.1
  614.4 14.2 %fusion.13 = bf16[128,1536]{1,0:T(8,128)(2,1)} fusion(bf16[128,8960]{1,0:T(8,128)(2,1)} %copy-done.2, bf16[8960,1536]{1,0:T(8,128)(2,1)} %param.17, bf16[128,1536]{1,0:T(8,128)(2,1)S(1)} %copy-done.4, bf16[128,1536]{1,0:T(8,128)(2,1)S(1)} %gather_fusion, pred[128]{0:T(512)(128)(4,1)S(1)} %get-tuple-element.6), kind=kOutput, calls=%fused_computation.25 | convolution fusion | flops 3524395008 | bytes 30998656 | tf_op jit(solution)/shard_map/dot_general | solution.py:59
  628.6 0.0 copy-done.1
  (5 shorter events, 0.0 us)
Async XLA Ops:
  0.0 48.5 %copy-start = (bf16[8,16,8960]{2,1,0:T(8,128)(2,1)S(1)}, bf16[8,16,8960]{2,1,0:T(8,128)(2,1)}, u32[]{:S(2)}) copy-start(bf16[8,16,8960]{2,1,0:T(8,128)(2,1)} %param.19) | copy-start | bytes 6881284
  2.9 30.8 %all-to-all-start = ((s32[16,32,1]{1,2,0:T(1,128)}), s32[16,32,1]{1,2,0:T(1,128)S(1)}, u32[]{:S(2)}, u32[]{:S(2)}) async-start(s32[16,32,1]{1,2,0:T(1,128)} %bitcast), calls=%async_computation | async-start | bytes 16384 | tf_op jit(solution)/shard_map/all_to_all | solution.py:41
  14.3 10.0 %copy-start.4 = (bf16[128,1536]{1,0:T(8,128)(2,1)S(1)}, bf16[128,1536]{1,0:T(8,128)(2,1)}, u32[]{:S(2)}) copy-start(bf16[128,1536]{1,0:T(8,128)(2,1)} %param.13) | copy-start | bytes 1179652
  14.3 10.0 %copy-start.5 = (bf16[128,1536,16]{1,2,0:T(8,128)(2,1)S(1)}, bf16[128,1536,16]{1,2,0:T(8,128)(2,1)}, u32[]{:S(2)}) copy-start(bf16[128,1536,16]{1,2,0:T(8,128)(2,1)} %param.18) | copy-start | bytes 18874372
  33.8 14.4 %all-to-all-start.1 = ((bf16[16,2,512]{2,1,0:T(2,128)(2,1)}), bf16[16,2,512]{2,1,0:T(2,128)(2,1)S(1)}, u32[]{:S(2)}, u32[]{:S(2)}) async-start(bf16[16,2,512]{2,1,0:T(2,128)(2,1)} %reshape.153), calls=%async_computation.1 | async-start | bytes 65536 | tf_op jit(solution)/shard_map/all_to_all | solution.py:46
  54.6 5.1 copy-start.6
  54.6 212.2 %all-to-all-start.2 = ((bf16[16,32,8960]{2,1,0:T(8,128)(2,1)}), bf16[16,32,8960]{2,1,0:T(8,128)(2,1)}, u32[]{:S(2)}, u32[]{:S(2)}) async-start(bf16[16,32,8960]{2,1,0:T(8,128)(2,1)} %bitcast.55), calls=%async_computation.2 | async-start | bytes 18350080 | tf_op jit(solution)/shard_map/all_to_all | solution.py:49
  266.8 214.8 %all-to-all-start.3 = ((bf16[16,32,8960]{2,1,0:T(8,128)(2,1)}), bf16[16,32,8960]{2,1,0:T(8,128)(2,1)}, u32[]{:S(2)}, u32[]{:S(2)}) async-start(bf16[16,32,8960]{2,1,0:T(8,128)(2,1)} %bitcast.54), calls=%async_computation.3 | async-start | bytes 18350080 | tf_op jit(solution)/shard_map/all_to_all | solution.py:50
  491.8 11.1 %copy-start.3 = (bf16[128,8960]{1,0:T(8,128)(2,1)S(1)}, bf16[128,8960]{1,0:T(8,128)(2,1)}, u32[]{:S(2)}) copy-start(bf16[128,8960]{1,0:T(8,128)(2,1)} %gather_fusion.2) | copy-start | bytes 6881284
  514.5 38.7 %copy-start.2 = (bf16[128,8960]{1,0:T(8,128)(2,1)}, bf16[128,8960]{1,0:T(8,128)(2,1)S(1)}, u32[]{:S(2)}) copy-start(bf16[128,8960]{1,0:T(8,128)(2,1)S(1)} %fusion.5) | copy-start | bytes 6881284
  614.4 14.2 %copy-start.1 = (bf16[8,16,8960]{2,1,0:T(8,128)(2,1)S(1)}, bf16[8,16,8960]{2,1,0:T(8,128)(2,1)}, u32[]{:S(2)}) copy-start(bf16[8,16,8960]{2,1,0:T(8,128)(2,1)} %param.19) | copy-start | bytes 6881284
where the time goes:
time: 639 us; the launch traced here: 629 us
  waiting for transfers between devices  404 us (63%)
  matrix products  107 us (17%)
  blocking collectives  57.2 us (9%)
  starting transfers between devices  31.4 us (5%)
  local copies, waits for them, and re-layouts  26 us (4%)
    all_to_all x1, waiting for transfers between devices, device_fn(): back_gate = lax.all_to_all(delta_gate, 'data', 0, 0, tiled=True)  201 us
    all_to_all x1, waiting for transfers between devices, device_fn(): back_up = lax.all_to_all(delta_up, 'data', 0, 0, tiled=True)  198 us
    dot_general x3, matrix products, pick_low(): jnp.einsum('tk,akr->tar', act_rows, a_all, preferred_element_type=jnp.flo...  56.2 us
    all_to_all x1, blocking collectives, device_fn(): lax.all_to_all(value_a7(recv_down, local_hot, b_down), 'data', 0, 0, tile...  42.2 us
    all_to_all x1, blocking collectives, device_fn(): recv_down = lax.all_to_all(send_down, 'data', 0, 0, tiled=True)  15 us
    dot_general x1, matrix products, device_fn(): jnp.dot(hid_act, w_down, preferred_element_type=jnp.float32)  14.2 us
    dot_general x3, matrix products, value_a7(): jnp.einsum('mar,arf->mf', spread, b_local, preferred_element_type=jnp.flo...  13.9 us
  transfers between devices with their start and end apart: 4, of which 3 were waited for; matrix products, arithmetic and copies ran while one was open for 6% of the time, Pallas kernels for 0%

commit v1 on v0

v1 whole, which is shorter than its diff:
```python
import jax
import jax.numpy as jnp
from jax import lax
from jax.sharding import PartitionSpec as P

scale_s = 2.0


def solution(mesh):
    groups = mesh.shape['data']
    row_spec = P(('rep', 'data'), None)
    tok_spec = P(('rep', 'data'))
    full_two = P(None, None)
    full_three = P(None, None, None)
    owned = P('data', None, None)

    def device_fn(hidden, adapter_id, w_gate, w_up, w_down, a_gate, b_gate, a_up, b_up, a_down, b_down):
        tok = hidden.shape[0]
        per_owner, rank, ff = b_gate.shape
        width = per_owner * rank
        cap = min(4 * tok // groups, tok // 2)
        me = lax.axis_index('data')
        owner = adapter_id // per_owner
        same = (owner[:, None] == owner[None, :]) & (jnp.arange(tok)[None, :] < jnp.arange(tok)[:, None])
        slot = owner * cap + jnp.sum(same.astype(jnp.int32), axis=1)
        place = (jnp.arange(groups * cap)[:, None] == slot[None, :])
        send_x = jnp.dot(place.astype(jnp.bfloat16), hidden, preferred_element_type=jnp.float32).astype(jnp.bfloat16)
        send_id = jnp.sum(jnp.where(place, (adapter_id % per_owner + 1)[None, :], 0), axis=1) - 1
        xs = lax.all_to_all(send_x, 'data', 0, 0, tiled=True)
        ids = lax.all_to_all(send_id, 'data', 0, 0, tiled=True)
        mask = (ids[:, None] == jnp.arange(width)[None, :] // rank)

        def mine(a):
            return lax.dynamic_slice_in_dim(a, me * per_owner, per_owner, 0)

        def delta(act, a, b):
            low = jnp.einsum('tk,akr->tar', act, mine(a), preferred_element_type=jnp.float32).reshape(-1, width)
            low = jnp.where(mask, low, 0.0).astype(jnp.bfloat16)
            full = jnp.dot(low, b.reshape(width, -1), preferred_element_type=jnp.float32)
            return (scale_s * full).astype(jnp.bfloat16).astype(jnp.float32)

        g = jnp.dot(xs, w_gate, preferred_element_type=jnp.float32) + delta(xs, a_gate, b_gate)
        u = jnp.dot(xs, w_up, preferred_element_type=jnp.float32) + delta(xs, a_up, b_up)
        h = (jax.nn.silu(g) * u).astype(jnp.bfloat16)
        y = jnp.dot(h, w_down, preferred_element_type=jnp.float32) + delta(h, a_down, b_down)
        out = (xs.astype(jnp.float32) + y).astype(jnp.bfloat16)
        back = lax.all_to_all(out, 'data', 0, 0, tiled=True)
        return lax.dot_general(place.astype(jnp.bfloat16), back, (((0,), (0,)), ((), ())), preferred_element_type=jnp.float32).astype(jnp.bfloat16)

    return jax.shard_map(device_fn, mesh=mesh, in_specs=(row_spec, tok_spec, full_two, full_two, full_two, full_three, owned, full_three, owned, full_three, owned), out_specs=row_spec, check_vma=False)
```

time: 639 us -> 208 us (0.33); the launches traced: 629 us -> 208 us
  waiting for transfers between devices: 404 us -> 37.2 us
  local copies, waits for them, and re-layouts: 26 us -> 6.12 us
  starting transfers between devices: 31.4 us -> 15.5 us
  blocking collectives: 57.2 us -> 44 us
    all_to_all x4 -> x2, waiting for transfers between devices: 404 us -> 37.2 us  [the longest x1 33 us: device_fn(): xs = lax.all_to_all(send_x, 'data', 0, 0, tiled=True)]
    gather x3 -> x0, local copies, waits for them, and re-layouts: 20 us -> none  [the longest x1 10.2 us: device_fn(): jnp.take(back_up, flat_slot, axis=0).astype(jnp.float32)]
    all_to_all x4 -> x2, starting transfers between devices: 31.4 us -> 15.5 us  [the longest x1 10.7 us: device_fn(): ids = lax.all_to_all(send_id, 'data', 0, 0, tiled=True)]
    all_to_all x2 -> x1, blocking collectives: 57.2 us -> 44 us  [device_fn(): back = lax.all_to_all(out, 'data', 0, 0, tiled=True)]
    dot_general x9 -> x8, matrix products: 107 us -> 96.1 us  [the longest x1 30.8 us: device_fn(): jnp.dot(xs, w_up, preferred_element_type=jnp.float32)]
    unnamed x0 -> x1, matrix products: none -> 6.78 us
  transfers between devices with their start and end apart: 4 -> 2, of which waited for: 3 -> 2; matrix products, arithmetic and copies ran while one was open for 6% -> 4% of each run, Pallas kernels for 0% -> 0%
where the time goes in v1:
time: 208 us
  matrix products  103 us (50%)
  blocking collectives  44 us (21%)
  waiting for transfers between devices  37.2 us (18%)
  starting transfers between devices  15.5 us (7%)
  local copies, waits for them, and re-layouts  6.12 us (3%)
    all_to_all x1, blocking collectives, device_fn(): back = lax.all_to_all(out, 'data', 0, 0, tiled=True)  44 us
    all_to_all x1, waiting for transfers between devices, device_fn(): xs = lax.all_to_all(send_x, 'data', 0, 0, tiled=True)  33 us
    dot_general x1, matrix products, device_fn(): jnp.dot(xs, w_up, preferred_element_type=jnp.float32)  30.8 us
    dot_general x1, matrix products, device_fn(): jnp.dot(xs, w_gate, preferred_element_type=jnp.float32)  23.8 us
    dot_general x3, matrix products, delta(): jnp.dot(low, b.reshape(width, -1), preferred_element_type=jnp.float32)  18.9 us
    dot_general x1, matrix products, device_fn(): jnp.dot(h, w_down, preferred_element_type=jnp.float32)  18.7 us
    all_to_all x1, starting transfers between devices, device_fn(): ids = lax.all_to_all(send_id, 'data', 0, 0, tiled=True)  10.7 us
    unnamed x1, matrix products  6.78 us
  transfers between devices with their start and end apart: 2, of which 2 were waited for; matrix products, arithmetic and copies ran while one was open for 4% of the time, Pallas kernels for 0%

profile of v1, /device:TPU:21, one launch (start us, length us, event | category | flops | bytes accessed | tf_op | source)
XLA Modules:
  0.0 207.6 jit_solution(10844016300829990461)
XLA Ops:
  0.0 0.0 copy-start
  0.0 0.8 fusion.21
  0.8 0.2 convert_reduce_fusion
  1.0 0.2 select_reduce_fusion
  1.2 0.7 sub.22
  1.9 10.7 %all-to-all-start.1 = ((s32[16,32,1]{1,2,0:T(1,128)}), s32[16,32,1]{1,2,0:T(1,128)S(1)}, u32[]{:S(2)}, u32[]{:S(2)}) async-start(s32[16,32,1]{1,2,0:T(1,128)} %bitcast.2), calls=%async_computation.1 | async-start | bytes 16384 | tf_op jit(solution)/shard_map/all_to_all | solution.py:30
  12.6 2.7 %convolution_convert_fusion = bf16[512,1536]{1,0:T(8,128)(2,1)} fusion(bf16[128,1536]{1,0:T(8,128)(2,1)} %param.11, s32[128]{0:T(128)S(1)} %multiply_add_fusion.1), kind=kOutput, calls=%fused_computation.9 | convolution fusion | flops 202178560 | bytes 1966592 | tf_op jit(solution)/shard_map/dot_general | solution.py:27
  15.3 4.2 %all-to-all-done.1 = s32[16,32,1]{1,2,0:T(1,128)S(1)} async-done(((s32[16,32,1]{1,2,0:T(1,128)}), s32[16,32,1]{1,2,0:T(1,128)S(1)}, u32[]{:S(2)}, u32[]{:S(2)}) %all-to-all-start.1) | async-done | bytes 2080 | tf_op jit(solution)/shard_map/all_to_all | solution.py:30
  19.5 4.8 %all-to-all-start = ((bf16[16,32,1536]{2,1,0:T(8,128)(2,1)}), bf16[16,32,1536]{2,1,0:T(8,128)(2,1)}, u32[]{:S(2)}, u32[]{:S(2)}) async-start(bf16[16,32,1536]{2,1,0:T(8,128)(2,1)} %bitcast.42), calls=%async_computation | async-start | bytes 3145728 | tf_op jit(solution)/shard_map/all_to_all | solution.py:29
  24.3 1.2 constant_dynamic-slice_fusion.1
  25.4 3.2 %constant_dynamic-slice_fusion = bf16[8,8960,16]{1,2,0:T(8,128)(2,1)} fusion(bf16[128,8960,16]{1,2,0:T(8,128)(2,1)} %param.20, s32[]{:T(128)S(6)} %select_n.49), kind=kLoop, calls=%fused_computation.49 | loop fusion | bytes 4587524 | tf_op jit(solution)/shard_map/dynamic_slice | solution.py:34
  28.7 0.5 broadcast.117
  29.2 0.7 reduce.3
  29.8 0.1 eq.56
  29.9 33.0 %all-to-all-done = bf16[16,32,1536]{2,1,0:T(8,128)(2,1)} async-done(((bf16[16,32,1536]{2,1,0:T(8,128)(2,1)}), bf16[16,32,1536]{2,1,0:T(8,128)(2,1)}, u32[]{:S(2)}, u32[]{:S(2)}) %all-to-all-start) | async-done | bytes 1572896 | tf_op jit(solution)/shard_map/all_to_all | solution.py:29
  62.9 23.8 %fusion.25 = f32[512,8960]{1,0:T(8,128)} fusion(bf16[512,1536]{1,0:T(8,128)(2,1)} %bitcast.1, bf16[1536,8960]{1,0:T(8,128)(2,1)} %param.13), kind=kOutput, calls=%fused_computation.57 | convolution fusion | flops 14092861440 | bytes 47448064 | tf_op jit(solution)/shard_map/dot_general | solution.py:42
  86.7 0.0 copy-done
  86.7 8.8 %multiply_convert_fusion.2 = bf16[512,8960]{1,0:T(8,128)(2,1)} fusion(bf16[128,8960]{1,0:T(8,128)(2,1)S(1)} %bitcast.41, bf16[512,1536]{1,0:T(8,128)(2,1)} %bitcast.1, bf16[128,1536]{1,0:T(8,128)(2,1)S(1)} %bitcast.47, s32[128]{0:T(128)S(1)} %and_select_fusion, s32[512]{0:T(512)S(1)} %eq.56), kind=kOutput, calls=%fused_computation.2 | convolution fusion | flops 1385103360 | bytes 13437440 | tf_op jit(solution)/shard_map/dot_general | solution.py:39
  95.5 9.5 %multiply_convert_fusion.1 = bf16[512,8960]{1,0:T(8,128)(2,1)} fusion(bf16[128,8960]{1,0:T(8,128)(2,1)} %bitcast.45, bf16[512,1536]{1,0:T(8,128)(2,1)} %bitcast.1, bf16[128,1536]{1,0:T(8,128)(2,1)S(1)} %bitcast.46, s32[128]{0:T(128)S(1)} %and_select_fusion, s32[512]{0:T(512)S(1)} %eq.56), kind=kOutput, calls=%fused_computation.1 | convolution fusion | flops 1385103360 | bytes 13437440 | tf_op jit(solution)/shard_map/dot_general | solution.py:39
  105.0 0.0 copy-start.2
  105.0 30.8 %multiply_convert_fusion = bf16[512,8960]{1,0:T(8,128)(2,1)} fusion(bf16[512,8960]{1,0:T(8,128)(2,1)} %multiply_convert_fusion.1, f32[512,8960]{1,0:T(8,128)} %fusion.25, bf16[512,8960]{1,0:T(8,128)(2,1)} %multiply_convert_fusion.2, bf16[512,1536]{1,0:T(8,128)(2,1)} %bitcast.1, bf16[1536,8960]{1,0:T(8,128)(2,1)} %param.14), kind=kOutput, calls=%fused_computation | convolution fusion | flops 14138736640 | bytes 74973184 | tf_op jit(solution)/shard_map/dot_general | solution.py:43
  135.8 0.0 copy-start.3
  135.8 0.0 copy-done.2
  135.8 0.0 slice-start
  135.8 0.0 slice-start.1
  135.8 6.8 %fusion.26 = f32[512,128]{0,1:S(1)} fusion(bf16[512,8960]{1,0:T(8,128)(2,1)} %multiply_convert_fusion, bf16[8960,128]{0,1:T(8,128)(2,1)S(1)} %bitcast.44), kind=kOutput, calls=%fused_computation.58 | convolution fusion | flops 1174405120 | bytes 11730944
  142.6 0.0 copy-done.3
  142.6 0.0 slice-start.2
  142.7 0.7 fusion.3
  143.3 0.0 slice-done
  143.3 0.0 slice-done.1
  143.3 0.4 slice-done.2
  143.8 0.0 copy-start.1
  143.8 18.7 %fusion.2 = bf16[512,1536]{1,0:T(8,128)(2,1)S(1)} fusion(bf16[512,1536]{1,0:T(8,128)(2,1)S(1)} %fusion.3, bf16[512,8960]{1,0:T(8,128)(2,1)S(1)} %bitcast.51, bf16[8960,1536]{1,0:T(8,128)(2,1)} %param.15, bf16[512,1536]{1,0:T(8,128)(2,1)} %bitcast.1), kind=kOutput, calls=%fused_computation.7 | convolution fusion | flops 14096793600 | bytes 41418752 | tf_op jit(solution)/shard_map/dot_general | solution.py:45
  162.4 44.0 %all_to_all.30 = bf16[16,32,1536]{2,1,0:T(8,128)(2,1)S(1)} all-to-all(bf16[16,32,1536]{2,1,0:T(8,128)(2,1)S(1)} %bitcast.48), channel_id=1, replica_groups=mesh['rep'=4,'data'=16] {'data'}, dimensions={0} | all-to-all | bytes 3145728 | tf_op jit(solution)/shard_map/all_to_all | solution.py:47
  206.4 1.2 convolution_convert_fusion.1
  207.6 0.0 copy-done.1
  (5 shorter events, 0.0 us)
Async XLA Ops:
  0.0 86.7 %copy-start = (bf16[8,16,8960]{2,1,0:T(8,128)(2,1)S(1)}, bf16[8,16,8960]{2,1,0:T(8,128)(2,1)}, u32[]{:S(2)}) copy-start(bf16[8,16,8960]{2,1,0:T(8,128)(2,1)} %param.17) | copy-start | bytes 6881284
  1.9 17.6 %all-to-all-start.1 = ((s32[16,32,1]{1,2,0:T(1,128)}), s32[16,32,1]{1,2,0:T(1,128)S(1)}, u32[]{:S(2)}, u32[]{:S(2)}) async-start(s32[16,32,1]{1,2,0:T(1,128)} %bitcast.2), calls=%async_computation.1 | async-start | bytes 16384 | tf_op jit(solution)/shard_map/all_to_all | solution.py:30
  19.5 43.4 %all-to-all-start = ((bf16[16,32,1536]{2,1,0:T(8,128)(2,1)}), bf16[16,32,1536]{2,1,0:T(8,128)(2,1)}, u32[]{:S(2)}, u32[]{:S(2)}) async-start(bf16[16,32,1536]{2,1,0:T(8,128)(2,1)} %bitcast.42), calls=%async_computation | async-start | bytes 3145728 | tf_op jit(solution)/shard_map/all_to_all | solution.py:29
  105.0 30.9 %copy-start.2 = (bf16[8,8960,16]{1,2,0:T(8,128)(2,1)S(1)}, bf16[8,8960,16]{1,2,0:T(8,128)(2,1)}, u32[]{:S(2)}) copy-start(bf16[8,8960,16]{1,2,0:T(8,128)(2,1)} %constant_dynamic-slice_fusion) | copy-start | bytes 6881284
  135.8 6.8 %copy-start.3 = (bf16[8,16,1536]{2,1,0:T(8,128)(2,1)S(1)}, bf16[8,16,1536]{2,1,0:T(8,128)(2,1)}, u32[]{:S(2)}) copy-start(bf16[8,16,1536]{2,1,0:T(8,128)(2,1)} %param.21) | copy-start | bytes 1179652
  135.8 7.5 %slice-start = ((s8[9175040]{0:T(1024)(128)(4,1)}), s8[4194304]{0:T(1024)(128)(4,1)S(1)}, s32[]{:S(2)}) async-start(s8[9175040]{0:T(1024)(128)(4,1)} %bitcast.50), calls=%async_computation.3 | async-start | bytes 8388608
  135.8 7.5 %slice-start.1 = ((s8[9175040]{0:T(1024)(128)(4,1)}), s8[4194304]{0:T(1024)(128)(4,1)S(1)}, s32[]{:S(2)}) async-start(s8[9175040]{0:T(1024)(128)(4,1)} %bitcast.50), calls=%async_computation.4 | async-start | bytes 8388608
  142.6 1.1 slice-start.2
  143.8 63.8 %copy-start.1 = (bf16[8,16,8960]{2,1,0:T(8,128)(2,1)S(1)}, bf16[8,16,8960]{2,1,0:T(8,128)(2,1)}, u32[]{:S(2)}) copy-start(bf16[8,16,8960]{2,1,0:T(8,128)(2,1)} %param.17) | copy-start | bytes 6881284

commit v2 on v1

v2 whole, which is shorter than its diff:
```python
import functools

import jax
import jax.numpy as jnp
from jax import lax
from jax.experimental import pallas as pl
from jax.experimental.pallas import tpu as pltpu
from jax.sharding import PartitionSpec as P

lora_scale = 2.0
col = 256
n_blocks = 7
n_slots = 4
same_rows = 32


def ring_order(chips):
    order = [0]
    for step in range(1, chips // 2):
        order += [step, chips - step]
    return order + [chips // 2]


def mlp_kernel(chips, rank, cross_rows, x_ref, id_ref, wg_ref, wu_ref, wd_ref, ag_ref, au_ref, ad_ref, bg_ref, bu_ref, bd_ref,
               o_ref, flag_ref, pg_ref, pu_ref, pd_ref,
               pool, xs, send, ret, hid, lowg, lowu, mask, ag, au, ad, bd, info,
               load_sem, wd_sem, small_sem, pair_sem, x_send, x_recv, info_send, info_recv, out_send, out_recv):
    order = ring_order(chips)
    position = {step: place for place, step in enumerate(order)}
    tok, depth = x_ref.shape
    width = bg_ref.shape[0]
    ff = wg_ref.shape[1]
    block = ff // n_blocks
    n_sub = block // col
    piece = depth + 2 * width
    used = 2 * n_sub * piece
    unit = same_rows + cross_rows
    rows = chips * unit
    half = rows // 2
    n_cols = depth // col
    per_slot = pool.shape[1] // ff
    f32, bf16 = jnp.float32, jnp.bfloat16

    me = lax.axis_index('data')
    core = lax.rem(me, 2)
    chip = me // 2
    partner = me + 1 - 2 * core
    targets = []
    for step in order:
        far = lax.rem(chip + step, chips)
        targets.append((2 * far + core, 2 * far + 1 - core))
    peers = [t for pair in targets for t in pair][1:]

    barrier = pltpu.get_barrier_semaphore()
    for peer in peers:
        pl.semaphore_signal(barrier, inc=1, device_id={'data': peer}, device_id_type=pl.DeviceIdType.MESH)

    def block_copies(b, slot, part):
        out = []
        for j in range(n_sub):
            cols = pl.ds(pl.multiple_of(b * block + j * col, col), col)
            for which, (w, own, far) in enumerate(((wg_ref, bg_ref, pg_ref), (wu_ref, bu_ref, pu_ref))):
                base = (2 * j + which) * piece
                if part != 'pair':
                    out.append((w.at[:, cols], pool.at[slot, pl.ds(base, depth)]))
                    out.append((own.at[:, cols], pool.at[slot, pl.ds(base + depth, width)]))
                if part != 'own':
                    out.append((far.at[:, cols], pool.at[slot, pl.ds(base + depth + width, width)]))
        for src, dst in out:
            pltpu.make_async_copy(src, dst, load_sem.at[slot]).start()

    def load_wait(slot):
        whole = pool.at[slot, pl.ds(0, used)]
        pltpu.make_async_copy(whole, whole, load_sem.at[slot]).wait()

    def remote(src, dst, s_sem, r_sem, dev):
        return pltpu.make_async_remote_copy(src_ref=src, dst_ref=dst, send_sem=s_sem, recv_sem=r_sem,
                                            device_id={'data': dev}, device_id_type=pl.DeviceIdType.MESH)

    for b in range(n_slots):
        block_copies(b, b, 'own')
    own_a = pl.ds(pl.multiple_of(me * width, width), width)
    far_a = pl.ds(pl.multiple_of(partner * width, width), width)
    for k, (src, dst) in enumerate(((ag_ref, ag), (au_ref, au), (ad_ref, ad))):
        pltpu.make_async_copy(src.at[own_a], dst.at[pl.ds(0, width)], small_sem.at[k]).start()
        pltpu.make_async_copy(src.at[far_a], dst.at[pl.ds(width, width)], small_sem.at[k]).start()
    pltpu.make_async_copy(bd_ref, bd.at[pl.ds(0, width)], small_sem.at[3]).start()

    ids = id_ref[...]
    tok_chip = ids // (2 * (width // rank))
    local = lax.rem(ids, 2 * (width // rank))
    step = lax.rem(tok_chip - chip + chips, chips)
    place = jnp.where(step < chips // 2, jnp.maximum(2 * step - 1, 0), jnp.where(step == chips // 2, chips - 1, 2 * (chips - step)))
    lanes = lax.broadcasted_iota(jnp.int32, (2 * chips, tok), 0)
    hot = (lanes == place).astype(f32)
    before = (lax.broadcasted_iota(jnp.int32, (tok, tok), 0) < lax.broadcasted_iota(jnp.int32, (tok, tok), 1))
    counts = jnp.dot(hot.astype(bf16), before.astype(f32).astype(bf16), preferred_element_type=f32)
    order_in = jnp.sum(hot * counts, axis=0, keepdims=True).astype(jnp.int32)
    over = order_in >= unit
    slot_of = jnp.where(over, rows + unit, place * unit + order_in)
    info[0] = slot_of * 32 + local
    perm = (lax.broadcasted_iota(jnp.int32, (rows, tok), 0) == slot_of).astype(f32).astype(bf16)
    send[...] = jnp.dot(perm, x_ref[...], preferred_element_type=f32).astype(bf16)
    xs[pl.ds(0, same_rows)] = send[pl.ds(0, same_rows)]

    pl.semaphore_wait(barrier, len(peers))

    for place_to, step_to in enumerate(order):
        seen = position[(chips - step_to) % chips]
        for kind in range(2):
            if place_to == 0 and kind == 0:
                continue
            remote(info.at[0], info.at[2 * seen + kind], info_send, info_recv, targets[place_to][kind]).start()
    pair_copies = [remote(src, dst, pair_sem.at[2 * k], pair_sem.at[2 * k + 1], partner)
                   for k, (src, dst) in enumerate(((bg_ref, pg_ref), (bu_ref, pu_ref), (bd_ref, pd_ref)))]
    for c in pair_copies:
        c.start()
    for place_to, step_to in enumerate(order):
        seen = position[(chips - step_to) % chips]
        for kind in range(2):
            if place_to == 0 and kind == 0:
                continue
            span = pl.ds(place_to * unit + kind * same_rows, cross_rows if kind else same_rows)
            land = pl.ds(seen * unit + kind * same_rows, cross_rows if kind else same_rows)
            remote(send.at[span], xs.at[land], x_send, x_recv.at[seen // (chips // 2)], targets[place_to][kind]).start()

    for c in pair_copies:
        c.wait()
    for b in range(n_slots):
        block_copies(b, b, 'pair')
    pltpu.make_async_copy(pd_ref, bd.at[pl.ds(width, width)], small_sem.at[3]).start()

    others = info.at[pl.ds(1, 2 * chips - 1)]
    pltpu.make_async_copy(others, others, info_recv).wait()
    flag = jnp.zeros((1, tok), jnp.int32)
    for seen, step_from in enumerate(order):
        theirs = position[(chips - step_from) % chips]
        for kind in range(2):
            code = info[2 * seen + kind]
            count = cross_rows if kind else same_rows
            slots = code // 32
            flag = jnp.maximum(flag, (slots >= rows).astype(jnp.int32))
            low_id = lax.rem(lax.rem(code, 32) + core * (width // rank), 2 * (width // rank))
            hit = lax.broadcasted_iota(jnp.int32, (count, tok), 0) + (theirs * unit + kind * same_rows) == slots
            pick = jnp.sum(jnp.where(hit, low_id + 1, 0), axis=1, keepdims=True)
            lane = lax.broadcasted_iota(jnp.int32, (count, 2 * width), 1) // rank + 1
            mask[pl.ds(seen * unit + kind * same_rows, count)] = (lane == pick).astype(f32).astype(bf16)
    flag_ref[...] = flag

    def low_rows(act, a, span):
        low = lax.dot_general(act, a[...], (((1,), (1,)), ((), ())), preferred_element_type=f32)
        return low.astype(bf16) * mask[span]

    def small_wait(k, dst):
        pltpu.make_async_copy(dst, dst, small_sem.at[k]).wait()

    def gate_up(b, span):
        slot = lax.rem(b, n_slots)
        act = xs[span]
        for j in range(n_sub):
            parts = []
            for which, low in enumerate((lowg, lowu)):
                base = (2 * j + which) * piece
                main = jnp.dot(act, pool[slot, pl.ds(base, depth)], preferred_element_type=f32)
                delta = jnp.dot(low[span], pool[slot, pl.ds(base + depth, 2 * width)], preferred_element_type=f32)
                parts.append(main + (lora_scale * delta).astype(bf16).astype(f32))
            gate, up = parts
            cols = pl.ds(pl.multiple_of(b * block + j * col, col), col)
            hid[span, cols] = (gate * jax.nn.sigmoid(gate) * up).astype(bf16)

    def x_wait(group, first):
        got = xs.at[pl.ds(first, (group + 1) * half - first)]
        pltpu.make_async_copy(got, got, x_recv.at[group]).wait()

    def wd_copy(j):
        slot = n_slots - 1 - j // per_slot
        start = (j % per_slot) * ff
        return pltpu.make_async_copy(wd_ref.at[:, pl.ds(pl.multiple_of(j * col, col), col)],
                                     pool.at[slot, pl.ds(start, ff)], wd_sem.at[j])

    near, far = pl.ds(0, half), pl.ds(half, half)
    small_wait(0, ag)
    small_wait(1, au)
    x_wait(0, same_rows)
    lowg[near] = low_rows(xs[near], ag, near)
    lowu[near] = low_rows(xs[near], au, near)

    @pl.loop(0, n_blocks)
    def _(b):
        load_wait(lax.rem(b, n_slots))
        gate_up(b, near)

        @pl.when(b < n_blocks - n_slots)
        def _():
            block_copies(b + n_slots, lax.rem(b, n_slots), 'all')

    x_wait(1, half)
    lowg[far] = low_rows(xs[far], ag, far)
    lowu[far] = low_rows(xs[far], au, far)

    @pl.loop(0, n_blocks)
    def _(i):
        b = n_blocks - 1 - i

        @pl.when(b < n_blocks - n_slots)
        def _():
            load_wait(lax.rem(b, n_slots))
        gate_up(b, far)

        @pl.when(i < n_blocks - n_slots)
        def _():
            block_copies(n_blocks - n_slots - 1 - i, lax.rem(b, n_slots), 'all')

        for k in range((n_cols + per_slot - 1) // per_slot):
            @pl.when(i == n_blocks - n_slots + k)
            def _():
                for j in range(k * per_slot, min((k + 1) * per_slot, n_cols)):
                    wd_copy(j).start()

    sent = send.at[pl.ds(same_rows, rows - same_rows)]
    pltpu.make_async_copy(sent, sent, x_send).wait()
    pltpu.make_async_copy(others, others, info_send).wait()
    small_wait(2, ad)
    small_wait(3, bd)
    every = pl.ds(0, rows)
    lowg[...] = low_rows(hid[...], ad, every)

    @pl.loop(0, n_cols)
    def _(j):
        slot = n_slots - 1 - j // per_slot
        start = pl.multiple_of(lax.rem(j, per_slot) * ff, 256)
        cols = pl.ds(pl.multiple_of(j * col, col), col)
        got = pool.at[slot, pl.ds(start, ff)]
        pltpu.make_async_copy(got, got, wd_sem.at[j]).wait()
        main = jnp.dot(hid[...], pool[slot, pl.ds(start, ff)], preferred_element_type=f32)
        delta = jnp.dot(lowg[...], bd[:, cols], preferred_element_type=f32)
        total = main + (lora_scale * delta).astype(bf16).astype(f32)
        send[:, cols] = (xs[:, cols].astype(f32) + total).astype(bf16)
        ret[pl.ds(0, same_rows), cols] = send[pl.ds(0, same_rows), cols]
        for seen in reversed(range(chips)):
            theirs = position[(chips - order[seen]) % chips]
            for kind in range(2):
                if seen == 0 and kind == 0:
                    continue
                count = cross_rows if kind else same_rows
                remote(send.at[pl.ds(seen * unit + kind * same_rows, count), cols],
                       ret.at[pl.ds(theirs * unit + kind * same_rows, count), cols],
                       out_send, out_recv, targets[seen][kind]).start()

    back = ret.at[pl.ds(same_rows, rows - same_rows)]
    pltpu.make_async_copy(back, back, out_recv).wait()
    o_ref[...] = lax.dot_general(perm, ret[...], (((0,), (0,)), ((), ())), preferred_element_type=f32).astype(bf16)
    pltpu.make_async_copy(sent, sent, out_send).wait()


def mlp_call(chips, rank, cross_rows, ident, x, ids, wg, wu, wd, ag, au, ad, bg, bu, bd):
    tok, depth = x.shape
    width = bg.shape[0]
    ff = wg.shape[1]
    rows = chips * (same_rows + cross_rows)
    n_sub = ff // n_blocks // col
    n_cols = depth // col
    slot_rows = max(2 * n_sub * (depth + 2 * width), ff)
    hbm, vmem = pl.BlockSpec(memory_space=pl.ANY), pl.BlockSpec(memory_space=pltpu.VMEM)
    bf16 = jnp.bfloat16
    dma = pltpu.SemaphoreType.DMA
    macs = rows * (3 * depth * ff + 2 * width * (2 * ff + depth) + 2 * width * (2 * depth + ff))
    return pl.pallas_call(
        functools.partial(mlp_kernel, chips, rank, cross_rows),
        out_shape=(jax.ShapeDtypeStruct((tok, depth), bf16), jax.ShapeDtypeStruct((1, tok), jnp.int32),
                   jax.ShapeDtypeStruct(bg.shape, bf16), jax.ShapeDtypeStruct(bu.shape, bf16), jax.ShapeDtypeStruct(bd.shape, bf16)),
        in_specs=[vmem, vmem] + [hbm] * 9,
        out_specs=(vmem, vmem, hbm, hbm, hbm),
        scratch_shapes=[
            pltpu.VMEM((n_slots, slot_rows, col), bf16),
            pltpu.VMEM((rows, depth), bf16), pltpu.VMEM((rows, depth), bf16), pltpu.VMEM((rows, depth), bf16),
            pltpu.VMEM((rows, ff), bf16),
            pltpu.VMEM((rows, 2 * width), bf16), pltpu.VMEM((rows, 2 * width), bf16), pltpu.VMEM((rows, 2 * width), bf16),
            pltpu.VMEM((2 * width, depth), bf16), pltpu.VMEM((2 * width, depth), bf16), pltpu.VMEM((2 * width, ff), bf16),
            pltpu.VMEM((2 * width, depth), bf16),
            pltpu.VMEM((2 * chips, 1, tok), jnp.int32),
            dma((n_slots,)), dma((n_cols,)), dma((4,)), dma((6,)), dma, dma((2,)), dma, dma, dma, dma,
        ],
        compiler_params=pltpu.CompilerParams(collective_id=ident, has_side_effects=True, vmem_limit_bytes=66_900_000),
        cost_estimate=pl.CostEstimate(flops=2 * macs, bytes_accessed=6 * depth * ff, transcendentals=rows * ff),
        name='mlp_%d' % cross_rows,
    )(x, ids, wg, wu, wd, ag, au, ad, bg, bu, bd)


def solution(mesh):
    groups = mesh.shape['data']
    row_spec = P(('rep', 'data'), None)
    tok_spec = P(('rep', 'data'))
    full_two = P(None, None)
    full_three = P(None, None, None)
    owned = P('data', None, None)

    def device_fn(hidden, adapter_id, w_gate, w_up, w_down, a_gate, b_gate, a_up, b_up, a_down, b_down):
        rank = b_gate.shape[1]

        def rank_rows(a):
            return jnp.swapaxes(a, 1, 2).reshape(-1, a.shape[1])

        def flat(b):
            return b.reshape(-1, b.shape[2])

        args = (hidden, adapter_id.reshape(1, -1), w_gate, w_up, w_down, rank_rows(a_gate), rank_rows(a_up), rank_rows(a_down),
                flat(b_gate), flat(b_up), flat(b_down))
        fast, flag = mlp_call(groups // 2, rank, same_rows // 2, 0, *args)[:2]
        return lax.cond(jnp.max(flag) > 0, lambda *a: mlp_call(groups // 2, rank, same_rows, 1, *a)[0], lambda *a: fast, *args)

    return jax.shard_map(device_fn, mesh=mesh, in_specs=(row_spec, tok_spec, full_two, full_two, full_two, full_three, owned, full_three, owned, full_three, owned), out_specs=row_spec, check_vma=False)
```

time: 208 us -> 93.2 us (0.45)
  matrix products: 103 us -> 0 us
  Pallas kernels: 0 us -> 89 us
  blocking collectives: 44 us -> 0 us
  waiting for transfers between devices: 37.2 us -> 0 us
  starting transfers between devices: 15.5 us -> 0 us
  local copies, waits for them, and re-layouts: 6.12 us -> 1.77 us
    dot_general x8 -> x0, matrix products: 96.1 us -> none  [the longest x1 30.8 us: device_fn(): jnp.dot(xs, w_up, preferred_element_type=jnp.float32)]
    pallas_call x0 -> x1, Pallas kernels: none -> 89 us  [mlp_call(): pl.pallas_call(functools.partial(mlp_kernel, chips, rank, cross_rows), ou...]
    all_to_all x1 -> x0, blocking collectives: 44 us -> none  [device_fn(): back = lax.all_to_all(out, 'data', 0, 0, tiled=True)]
    all_to_all x2 -> x0, waiting for transfers between devices: 37.2 us -> none  [the longest x1 33 us: device_fn(): xs = lax.all_to_all(send_x, 'data', 0, 0, tiled=True)]
    all_to_all x2 -> x0, starting transfers between devices: 15.5 us -> none  [the longest x1 10.7 us: device_fn(): ids = lax.all_to_all(send_id, 'data', 0, 0, tiled=True)]
    unnamed x1 -> x0, matrix products: 6.78 us -> none
    dynamic_slice x2 -> x0, local copies, waits for them, and re-layouts: 4.39 us -> none  [mine(): return lax.dynamic_slice_in_dim(a, me * per_owner, per_owner, 0)]
  transfers between devices with their start and end apart: 2 -> 0, of which waited for: 2 -> 0; matrix products, arithmetic and copies ran while one was open for 4% -> 0% of each run, Pallas kernels for 0% -> 0%
where the time goes in v2:
time: 93.2 us; the launch traced here: 92.9 us
  Pallas kernels  89 us (95%)
  local copies, waits for them, and re-layouts  1.77 us (2%)
  other arithmetic  1.3 us (1%)
    pallas_call x1, Pallas kernels, mlp_call(): pl.pallas_call(functools.partial(mlp_kernel, chips, rank, cross_rows), ou...  89 us

profile of v2, /device:TPU:21, one launch (start us, length us, event | category | flops | bytes accessed | tf_op | source)
XLA Modules:
  0.0 92.9 jit_solution(1800910827450745518)
XLA Ops:
  0.0 0.0 copy-start
  0.0 89.0 %mlp_16.1 = (bf16[128,1536]{1,0:T(8,128)(2,1)}, s32[1,128]{1,0:T(1,128)}, bf16[128,8960]{1,0:T(8,128)(2,1)}, bf16[128,8960]{1,0:T(8,128)(2,1)}, bf16[128,1536]{1,0:T(8,128)(2,1)}) custom-call(bf16[128,1536]{1,0:T(8,128)(2,1)} %x_ref.1, s32[1,128]{1,0:T(1,128)} %bitcast.25, bf16[1536,8960]{1,0:T(8,128)(2,1)} %wg_ref.1, bf16[1536,8960]{1,0:T(8,128)(2,1)} %wu_ref.1, ...), custom_call_target="tpu_custom_call" | custom-call | flops 37899730944 | bytes 82575360 | tf_op jit(solution)/shard_map/mlp_16/pallas_call | solution.py:268
  89.0 1.3 %reduce_max.9 = s32[]{:T(128)} reduce(s32[1,128]{1,0:T(1,128)} %get-tuple-element.45, s32[]{:T(128)} %constant.0.clone.1), dimensions={0,1}, to_apply=%region_0.0 | reduce | flops 127 | bytes 520 | tf_op jit(solution)/shard_map/reduce_max | solution.py:310
  90.9 0.0 copy-done
  90.9 0.2 conditional.1
  91.1 1.8 %copy.17 = bf16[128,1536]{1,0:T(8,128)(2,1)} copy(bf16[128,1536]{1,0:T(8,128)(2,1)} %get-tuple-element.47) | data formatting | bytes 786432
Async XLA Ops:
  0.0 90.9 %copy-start = (s32[128]{0:T(128)S(1)}, s32[128]{0:T(128)}, u32[]{:S(2)}) copy-start(s32[128]{0:T(128)} %param.14) | copy-start | bytes 1540

commit v3 on v2

--- a/solution.py
+++ b/solution.py
@@ -287,6 +287,368 @@
     )(x, ids, wg, wu, wd, ag, au, ad, bg, bu, bd)
 
 
+base_rows = 16
+extra_rows = 32
+
+
+def lane_kernel(chips, rank, x_ref, id_ref, wg_ref, wu_ref, wd_ref, ag_ref, au_ref, ad_ref, bg_ref, bu_ref, bd_ref,
+                o_ref, flag_ref, pg_ref, pu_ref, pd_ref,
+                pool, xs, send, stage, ret, hid, lowg, lowu, mask, valid, ag, au, ad, bd, info, merge,
+                load_sem, wd_sem, small_sem, pair_send, pair_recv, base_send, base_recv, extra_send, extra_recv,
+                info_send, info_recv, out_send, out_recv, merge_send, merge_recv):
+    order = ring_order(chips)
+    position = {step: place for place, step in enumerate(order)}
+    tok, depth = x_ref.shape
+    width = bg_ref.shape[0]
+    ff = wg_ref.shape[1]
+    block = ff // n_blocks
+    n_sub = block // col
+    piece = depth + 2 * width
+    used = 2 * n_sub * piece
+    per_chip = 2 * (width // rank)
+    n_cols = depth // col
+    per_slot = pool.shape[1] // ff
+    last = chips // 2
+    near_base, near_extra = last + 1, 3
+    first_extra = near_base * base_rows
+    end_extra = first_extra + chips * extra_rows
+    rows = end_extra + (chips - near_base) * base_rows
+    split = first_extra + near_extra * extra_rows
+    slots_base = chips * base_rows
+    slots = slots_base + extra_rows
+    part = extra_rows // 2
+    f32, bf16 = jnp.float32, jnp.bfloat16
+
+    def base_at(seen):
+        return seen * base_rows if seen < near_base else end_extra + (seen - near_base) * base_rows
+
+    def extra_at(seen):
+        return first_extra + seen * extra_rows
+
+    me = lax.axis_index('data')
+    core = lax.rem(me, 2)
+    chip = me // 2
+    partner = me + 1 - 2 * core
+    lane = [2 * lax.rem(chip + step, chips) + core for step in order]
+    cross = [2 * lax.rem(chip + step, chips) + 1 - core for step in order]
+    up, down = lane[1], lane[2]
+    peers = lane[1:] + cross
+
+    barrier = pltpu.get_barrier_semaphore()
+    for peer in peers:
+        pl.semaphore_signal(barrier, inc=1, device_id={'data': peer}, device_id_type=pl.DeviceIdType.MESH)
+
+    def block_copies(b, slot, which_part):
+        for j in range(n_sub):
+            cols = pl.ds(pl.multiple_of(b * block + j * col, col), col)
+            for which, (w, own, far) in enumerate(((wg_ref, bg_ref, pg_ref), (wu_ref, bu_ref, pu_ref))):
+                base = (2 * j + which) * piece
+                todo = []
+                if which_part != 'pair':
+                    todo += [(w, base, depth), (own, base + depth, width)]
+                if which_part != 'own':
+                    todo += [(far, base + depth + width, width)]
+                for src, start, count in todo:
+                    pltpu.make_async_copy(src.at[:, cols], pool.at[slot, pl.ds(start, count)], load_sem.at[slot]).start()
+
+    def load_wait(slot):
+        whole = pool.at[slot, pl.ds(0, used)]
+        pltpu.make_async_copy(whole, whole, load_sem.at[slot]).wait()
+
+    def remote(src, dst, s_sem, r_sem, dev):
+        return pltpu.make_async_remote_copy(src_ref=src, dst_ref=dst, send_sem=s_sem, recv_sem=r_sem,
+                                            device_id={'data': dev}, device_id_type=pl.DeviceIdType.MESH)
+
+    def await_bytes(ref, sem):
+        pltpu.make_async_copy(ref, ref, sem).wait()
+
+    for b in range(n_slots):
+        block_copies(b, b, 'own')
+    own_a = pl.ds(pl.multiple_of(me * width, width), width)
+    far_a = pl.ds(pl.multiple_of(partner * width, width), width)
+    for k, (src, dst) in enumerate(((ag_ref, ag), (au_ref, au), (ad_ref, ad))):
+        pltpu.make_async_copy(src.at[own_a], dst.at[pl.ds(0, width)], small_sem.at[k]).start()
+        pltpu.make_async_copy(src.at[far_a], dst.at[pl.ds(width, width)], small_sem.at[k]).start()
+    pltpu.make_async_copy(bd_ref, bd.at[pl.ds(0, width)], small_sem.at[3]).start()
+
+    ids = id_ref[...]
+    step = lax.rem(ids // per_chip - chip + chips, chips)
+    place = jnp.where(step < last, jnp.maximum(2 * step - 1, 0), jnp.where(step == last, chips - 1, 2 * (chips - step)))
+    hot = (lax.broadcasted_iota(jnp.int32, (2 * chips, tok), 0) == place).astype(f32)
+    before = (lax.broadcasted_iota(jnp.int32, (tok, tok), 0) < lax.broadcasted_iota(jnp.int32, (tok, tok), 1)).astype(f32).astype(bf16)
+    counts = jnp.dot(hot.astype(bf16), before, preferred_element_type=f32)
+    order_in = jnp.sum(hot * counts, axis=0, keepdims=True)
+    spill = jnp.broadcast_to((order_in >= base_rows).astype(f32), (2 * chips, tok))
+    spilled = jnp.dot(spill.astype(bf16), before, preferred_element_type=f32)[:1].astype(jnp.int32)
+    order_in = order_in.astype(jnp.int32)
+    slot_of = jnp.where(order_in < base_rows, place * base_rows + order_in, slots_base + spilled)
+    info[0] = slot_of * (per_chip * chips) + ids
+    perm = (lax.broadcasted_iota(jnp.int32, (slots, tok), 0) == slot_of).astype(f32).astype(bf16)
+    send[...] = jnp.dot(perm, x_ref[...], preferred_element_type=f32).astype(bf16)
+    xs[pl.ds(0, base_rows)] = send[pl.ds(0, base_rows)]
+    xs[pl.ds(extra_at(0), extra_rows)] = send[pl.ds(slots_base, extra_rows)]
+
+    pl.semaphore_wait(barrier, len(peers))
+
+    for to, step_to in enumerate(order):
+        seen = position[(chips - step_to) % chips]
+        if to:
+            remote(info.at[0], info.at[2 * seen], info_send, info_recv, lane[to]).start()
+        remote(info.at[0], info.at[2 * seen + 1], info_send, info_recv, cross[to]).start()
+
+    def pass_on(hop, start):
+        for way, dev in ((0, up), (1, down)):
+            src_seen = 0 if hop == 0 else position[(chips - hop) % chips if way == 0 else hop]
+            dst_seen = position[(chips - hop - 1) % chips if way == 0 else hop + 1]
+            first, count = (way * part, part) if hop == last - 1 else (0, extra_rows)
+            src = send.at[pl.ds(slots_base, extra_rows)] if hop == 0 else xs.at[pl.ds(extra_at(src_seen) + first, count)]
+            if hop and start:
+                whole = xs.at[pl.ds(extra_at(src_seen), extra_rows)]
+                await_bytes(whole, extra_recv.at[way, hop - 1])
+            remote(src, xs.at[pl.ds(extra_at(dst_seen) + first, count)], extra_send, extra_recv.at[way, hop], dev).start()
+
+    pass_on(0, True)
+    pair_copies = []
+    for b in range(n_blocks):
+        cols = pl.ds(b * block, block)
+        pair_copies.append(remote(bg_ref.at[:, cols], pg_ref.at[:, cols], pair_send.at[2 * b], pair_recv.at[2 * b], partner))
+        pair_copies.append(remote(bu_ref.at[:, cols], pu_ref.at[:, cols], pair_send.at[2 * b + 1], pair_recv.at[2 * b + 1], partner))
+    pair_copies.append(remote(bd_ref, pd_ref, pair_send.at[2 * n_blocks], pair_recv.at[2 * n_blocks], partner))
+    for c in pair_copies:
+        c.start()
+    for to, step_to in enumerate(order):
+        seen = position[(chips - step_to) % chips]
+        if to:
+            remote(send.at[pl.ds(to * base_rows, base_rows)], xs.at[pl.ds(base_at(seen), base_rows)],
+                   base_send, base_recv.at[int(seen >= near_base)], lane[to]).start()
+
+    def pair_wait(b):
+        cols = pl.ds(pl.multiple_of(b * block, col), block)
+        await_bytes(pg_ref.at[:, cols], pair_recv.at[2 * b])
+        await_bytes(pu_ref.at[:, cols], pair_recv.at[2 * b + 1])
+
+    await_bytes(info.at[pl.ds(1, 2 * chips - 1)], info_recv)
+    flag = jnp.zeros((1, tok), jnp.int32)
+    for other in range(2 * chips):
+        flag = jnp.maximum(flag, (info[other] // (per_chip * chips) >= slots).astype(jnp.int32))
+    flag_ref[...] = flag
+    for seen, step_from in enumerate(order):
+        theirs = position[(chips - step_from) % chips]
+        code = info[2 * seen]
+        theirs_slot = code // (per_chip * chips)
+        adapter = lax.rem(code, per_chip * chips)
+        pick_id = jnp.where(adapter // per_chip == chip, lax.rem(lax.rem(adapter, per_chip) + core * (width // rank), per_chip) + 1, 0)
+        for at, start, count in ((base_at(seen), theirs * base_rows, base_rows), (extra_at(seen), slots_base, extra_rows)):
+            hit = lax.broadcasted_iota(jnp.int32, (count, tok), 0) + start == theirs_slot
+            pick = jnp.sum(jnp.where(hit, pick_id, 0), axis=1, keepdims=True)
+            lane_id = lax.broadcasted_iota(jnp.int32, (count, 2 * width), 1) // rank + 1
+            mask[pl.ds(at, count)] = (lane_id == pick).astype(f32).astype(bf16)
+            if count == extra_rows:
+                valid[pl.ds(at - first_extra, count)] = jnp.broadcast_to((pick > 0).astype(f32), (count, col))
+
+    pair_wait(0)
+    block_copies(0, 0, 'pair')
+    pass_on(1, True)
+
+    def low_rows(act, a, span):
+        low = lax.dot_general(act, a[...], (((1,), (1,)), ((), ())), preferred_element_type=f32)
+        return low.astype(bf16) * mask[span]
+
+    def gate_up(b, span):
+        slot = lax.rem(b, n_slots)
+        act = xs[span]
+        for j in range(n_sub):
+            parts = []
+            for which, low in enumerate((lowg, lowu)):
+                base = (2 * j + which) * piece
+                main = jnp.dot(act, pool[slot, pl.ds(base, depth)], preferred_element_type=f32)
+                delta = jnp.dot(low[span], pool[slot, pl.ds(base + depth, 2 * width)], preferred_element_type=f32)
+                parts.append(main + (lora_scale * delta).astype(bf16).astype(f32))
+            gate, up_act = parts
+            cols = pl.ds(pl.multiple_of(b * block + j * col, col), col)
+            hid[span, cols] = (gate * jax.nn.sigmoid(gate) * up_act).astype(bf16)
+
+    def wd_copy(j):
+        slot = n_slots - 1 - j // per_slot
+        start = (j % per_slot) * ff
+        return pltpu.make_async_copy(wd_ref.at[:, pl.ds(pl.multiple_of(j * col, col), col)],
+                                     pool.at[slot, pl.ds(start, ff)], wd_sem.at[j])
+
+    near, far = pl.ds(0, split), pl.ds(split, rows - split)
+    await_bytes(ag, small_sem.at[0])
+    await_bytes(au, small_sem.at[1])
+    await_bytes(xs.at[pl.ds(base_rows, first_extra - base_rows)], base_recv.at[0])
+    for b in range(1, n_slots):
+        pair_wait(b)
+        block_copies(b, b, 'pair')
+    lowg[near] = low_rows(xs[near], ag, near)
+    lowu[near] = low_rows(xs[near], au, near)
+
+    @pl.loop(0, n_blocks)
+    def _(b):
+        load_wait(lax.rem(b, n_slots))
+        gate_up(b, near)
+        for hop in range(2, last):
+            @pl.when(b == 2 * hop - 3)
+            def _():
+                pass_on(hop, True)
+
+        @pl.when(b < n_blocks - n_slots)
+        def _():
+            pair_wait(b + n_slots)
+            block_copies(b + n_slots, lax.rem(b, n_slots), 'all')
+
+    final = position[last]
+    for way in range(2):
+        await_bytes(xs.at[pl.ds(extra_at(final) + way * part, part)], extra_recv.at[way, last - 1])
+    await_bytes(xs.at[pl.ds(end_extra, rows - end_extra)], base_recv.at[1])
+    lowg[far] = low_rows(xs[far], ag, far)
+    lowu[far] = low_rows(xs[far], au, far)
+
+    @pl.loop(0, n_blocks)
+    def _(i):
+        b = n_blocks - 1 - i
+
+        @pl.when(b < n_blocks - n_slots)
+        def _():
+            load_wait(lax.rem(b, n_slots))
+        gate_up(b, far)
+
+        @pl.when(i < n_blocks - n_slots)
+        def _():
+            block_copies(n_blocks - n_slots - 1 - i, lax.rem(b, n_slots), 'all')
+
+        for k in range((n_cols + per_slot - 1) // per_slot):
+            @pl.when(i == n_blocks - n_slots + k)
+            def _():
+                for j in range(k * per_slot, min((k + 1) * per_slot, n_cols)):
+                    wd_copy(j).start()
+
+    await_bytes(pd_ref, pair_recv.at[2 * n_blocks])
+    pd_load = pltpu.make_async_copy(pd_ref, bd.at[pl.ds(width, width)], small_sem.at[3])
+    pd_load.start()
+    await_bytes(ad, small_sem.at[2])
+    lowg[...] = low_rows(hid[...], ad, pl.ds(0, rows))
+    await_bytes(bd, small_sem.at[3])
+
+    def down_cols(j, pieces):
+        slot = n_slots - 1 - j // per_slot
+        start = pl.multiple_of(lax.rem(j, per_slot) * ff, col)
+        cols = pl.ds(pl.multiple_of(j * col, col), col)
+
+        def take(ref, c):
+            got = [ref[p, c] for p in pieces]
+            return got[0] if len(got) == 1 else jnp.concatenate(got, axis=0)
+        every = slice(None)
+        main = jnp.dot(take(hid, every), pool[slot, pl.ds(start, ff)], preferred_element_type=f32)
+        delta = jnp.dot(take(lowg, every), bd[:, cols], preferred_element_type=f32)
+        return take(xs, cols).astype(f32) + (main + (lora_scale * delta).astype(bf16).astype(f32)), cols
+
+    def merge_step(hop, j):
+        cols = pl.ds(pl.multiple_of(j * col, col), col)
+        for way, dev in ((0, up), (1, down)):
+            home = position[last - hop if way == 0 else (chips - last + hop) % chips]
+            at = extra_at(home)
+            first, count = (way * part, part) if hop == 0 else (0, extra_rows)
+            if hop:
+                f, c = (way * part, part) if hop == 1 else (0, extra_rows)
+                got = merge.at[way, hop - 1, pl.ds(f, c), cols]
+                await_bytes(got, merge_recv.at[way, hop - 1, j])
+                mine = pl.ds(at + f, c)
+                stage[mine, cols] = stage[mine, cols] + merge[way, hop - 1, pl.ds(f, c), cols]
+            remote(stage.at[pl.ds(at + first, count), cols], merge.at[way, hop, pl.ds(first, count), cols],
+                   merge_send, merge_recv.at[way, hop, j], dev).start()
+
+    def merge_steps(turn):
+        for hop in range(1, last):
+            t = turn - 2 * hop
+
+            @pl.when((t >= 0) & (t < n_cols))
+            def _():
+                merge_step(hop, t)
+
+    @pl.loop(0, n_cols)
+    def _(j):
+        cols = pl.ds(pl.multiple_of(j * col, col), col)
+        got = pool.at[n_slots - 1 - j // per_slot, pl.ds(pl.multiple_of(lax.rem(j, per_slot) * ff, col), ff)]
+        await_bytes(got, wd_sem.at[j])
+        total, _ = down_cols(j, [pl.ds(first_extra, chips * extra_rows)])
+        stage[pl.ds(first_extra, chips * extra_rows), cols] = jnp.where(valid[...] > 0, total, 0.0).astype(bf16)
+        merge_step(0, j)
+        merge_steps(j)
+
+    @pl.loop(0, n_cols)
+    def _(j):
+        total, cols = down_cols(j, [pl.ds(0, first_extra), pl.ds(end_extra, rows - end_extra)])
+        total = total.astype(bf16)
+        stage[pl.ds(0, first_extra), cols] = total[:first_extra]
+        stage[pl.ds(end_extra, rows - end_extra), cols] = total[first_extra:]
+        ret[pl.ds(0, base_rows), cols] = total[:base_rows]
+        for seen in reversed(range(1, chips)):
+            theirs = position[(chips - order[seen]) % chips]
+            remote(stage.at[pl.ds(base_at(seen), base_rows), cols], ret.at[pl.ds(theirs * base_rows, base_rows), cols],
+                   out_send, out_recv, lane[seen]).start()
+        merge_steps(j + n_cols)
+
+    for turn in range(2 * n_cols, n_cols + 2 * (last - 1)):
+        for hop in range(1, last):
+            if 0 <= turn - 2 * hop < n_cols:
+                merge_step(hop, turn - 2 * hop)
+    for j in range(n_cols):
+        cols = pl.ds(j * col, col)
+        for way in range(2):
+            await_bytes(merge.at[way, last - 1, pl.ds(0, extra_rows), cols], merge_recv.at[way, last - 1, j])
+    ret[pl.ds(slots_base, extra_rows)] = stage[pl.ds(extra_at(0), extra_rows)] + (merge[0, last - 1] + merge[1, last - 1])
+    await_bytes(ret.at[pl.ds(base_rows, slots_base - base_rows)], out_recv)
+    o_ref[...] = lax.dot_general(perm, ret[...], (((0,), (0,)), ((), ())), preferred_element_type=f32).astype(bf16)
+
+    for c in pair_copies:
+        c.wait_send()
+    await_bytes(info.at[pl.ds(1, 2 * chips - 1)], info_send)
+    await_bytes(send.at[pl.ds(base_rows, slots_base - base_rows)], base_send)
+    await_bytes(xs.at[pl.ds(0, (2 * last - 1) * extra_rows)], extra_send)
+    await_bytes(ret.at[pl.ds(base_rows, slots_base - base_rows)], out_send)
+    await_bytes(stage.at[pl.ds(0, (2 * last - 1) * extra_rows)], merge_send)
+
+
+def lane_call(chips, rank, ident, x, ids, wg, wu, wd, ag, au, ad, bg, bu, bd):
+    tok, depth = x.shape
+    width = bg.shape[0]
+    ff = wg.shape[1]
+    rows = chips * (base_rows + extra_rows)
+    slots = chips * base_rows + extra_rows
+    n_sub = ff // n_blocks // col
+    n_cols = depth // col
+    slot_rows = max(2 * n_sub * (depth + 2 * width), ff)
+    hbm, vmem = pl.BlockSpec(memory_space=pl.ANY), pl.BlockSpec(memory_space=pltpu.VMEM)
+    bf16 = jnp.bfloat16
+    dma = pltpu.SemaphoreType.DMA
+    macs = rows * (3 * depth * ff + 2 * width * (2 * ff + depth) + 2 * width * (2 * depth + ff))
+    low = pltpu.VMEM((rows, 2 * width), bf16)
+    a_buf = pltpu.VMEM((2 * width, depth), bf16)
+    return pl.pallas_call(
+        functools.partial(lane_kernel, chips, rank),
+        out_shape=(jax.ShapeDtypeStruct((tok, depth), bf16), jax.ShapeDtypeStruct((1, tok), jnp.int32),
+                   jax.ShapeDtypeStruct(bg.shape, bf16), jax.ShapeDtypeStruct(bu.shape, bf16), jax.ShapeDtypeStruct(bd.shape, bf16)),
+        in_specs=[vmem, vmem] + [hbm] * 9,
+        out_specs=(vmem, vmem, hbm, hbm, hbm),
+        scratch_shapes=[
+            pltpu.VMEM((n_slots, slot_rows, col), bf16),
+            pltpu.VMEM((rows, depth), bf16), pltpu.VMEM((slots, depth), bf16), pltpu.VMEM((rows, depth), bf16), pltpu.VMEM((slots, depth), bf16),
+            pltpu.VMEM((rows, ff), bf16),
+            low, low, low, pltpu.VMEM((chips * extra_rows, col), jnp.float32),
+            a_buf, a_buf, pltpu.VMEM((2 * width, ff), bf16), a_buf,
+            pltpu.VMEM((2 * chips, 1, tok), jnp.int32),
+            pltpu.VMEM((2, chips // 2, extra_rows, depth), bf16),
+            dma((n_slots,)), dma((n_cols,)), dma((4,)), dma((2 * n_blocks + 1,)), dma((2 * n_blocks + 1,)), dma, dma((2,)), dma, dma((2, chips // 2)),
+            dma, dma, dma, dma, dma, dma((2, chips // 2, n_cols)),
+        ],
+        compiler_params=pltpu.CompilerParams(collective_id=ident, has_side_effects=True, vmem_limit_bytes=66_900_000),
+        cost_estimate=pl.CostEstimate(flops=2 * macs, bytes_accessed=6 * depth * ff, transcendentals=rows * ff),
+        name='mlp_lane',
+    )(x, ids, wg, wu, wd, ag, au, ad, bg, bu, bd)
+
+
 def solution(mesh):
     groups = mesh.shape['data']
     row_spec = P(('rep', 'data'), None)
@@ -306,7 +668,7 @@
 
         args = (hidden, adapter_id.reshape(1, -1), w_gate, w_up, w_down, rank_rows(a_gate), rank_rows(a_up), rank_rows(a_down),
                 flat(b_gate), flat(b_up), flat(b_down))
-        fast, flag = mlp_call(groups // 2, rank, same_rows // 2, 0, *args)[:2]
+        fast, flag = lane_call(groups // 2, rank, 0, *args)[:2]
         return lax.cond(jnp.max(flag) > 0, lambda *a: mlp_call(groups // 2, rank, same_rows, 1, *a)[0], lambda *a: fast, *args)
 
     return jax.shard_map(device_fn, mesh=mesh, in_specs=(row_spec, tok_spec, full_two, full_two, full_two, full_three, owned, full_three, owned, full_three, owned), out_specs=row_spec, check_vma=False)

time: 93.2 us -> 86.7 us (0.930)
  the two profiles are of different devices: /device:TPU:21 before, /device:TPU:28 now
where the time goes in v3:
time: 86.7 us; the launch traced here: 86.6 us
  Pallas kernels  82.6 us (95%)
  local copies, waits for them, and re-layouts  1.77 us (2%)
  other arithmetic  1.3 us (1%)
    pallas_call x1, Pallas kernels, lane_call(): pl.pallas_call(functools.partial(lane_kernel, chips, rank), out_shape=(ja...  82.6 us
    unnamed x3, local copies, waits for them, and re-layouts  1.77 us

profile of v3, /device:TPU:28, one launch (start us, length us, event | category | flops | bytes accessed | tf_op | source)
XLA Modules:
  0.0 86.6 jit_solution(5336013967602989021)
XLA Ops:
  0.0 0.0 copy-start
  0.0 82.6 %mlp_lane.1 = (bf16[128,1536]{1,0:T(8,128)(2,1)}, s32[1,128]{1,0:T(1,128)}, bf16[128,8960]{1,0:T(8,128)(2,1)}, bf16[128,8960]{1,0:T(8,128)(2,1)}, bf16[128,1536]{1,0:T(8,128)(2,1)}) custom-call(bf16[128,1536]{1,0:T(8,128)(2,1)} %x_ref.1, s32[1,128]{1,0:T(1,128)} %bitcast.25, bf16[1536,8960]{1,0:T(8,128)(2,1)} %wg_ref.1, bf16[1536,8960]{1,0:T(8,128)(2,1)} %wu_ref.1, ...), custom_call_target="tpu_custom_call" | custom-call | flops 37899730944 | bytes 82575360 | tf_op jit(solution)/shard_map/mlp_lane/pallas_call | solution.py:629
  82.6 1.3 %reduce_max.9 = s32[]{:T(128)} reduce(s32[1,128]{1,0:T(1,128)} %get-tuple-element.45, s32[]{:T(128)} %constant.0.clone.1), dimensions={0,1}, to_apply=%region_0.0 | reduce | flops 127 | bytes 520 | tf_op jit(solution)/shard_map/reduce_max | solution.py:672
  84.6 0.0 copy-done
  84.6 0.2 conditional.1
  84.8 1.8 %copy.17 = bf16[128,1536]{1,0:T(8,128)(2,1)} copy(bf16[128,1536]{1,0:T(8,128)(2,1)} %get-tuple-element.47) | data formatting | bytes 786432
Async XLA Ops:
  0.0 84.6 %copy-start = (s32[128]{0:T(128)S(1)}, s32[128]{0:T(128)}, u32[]{:S(2)}) copy-start(s32[128]{0:T(128)} %param.14) | copy-start | bytes 1540
